TPU v7x, 32 devices: a whole 2x2x4 slice. The times are simulated.
32 devices in a mesh: blk: 8 (over y, x, core), heads: 4 (over z).
Axes of the slice: x: 2, y: 2, z: 4, core: 2. Of those that a mesh axis runs over, the one named last changes fastest.
Arguments:
- queries: bfloat16 [2048, 4096], P('blk', 'heads'), may hold values from -5 to 5
- keys: bfloat16 [2048, 1024], P('blk', 'heads'), may hold values from -5 to 5
- values: bfloat16 [2048, 1024], P('blk', 'heads'), may hold values from -6 to 6
- doc_ids: int32 [2048], P('blk'), may hold values from 0 to 7, never falling along the last dimension, each value on 1 to 1024 neighbouring positions
Outputs:
- attended: bfloat16 [2048, 4096], P('blk', 'heads')
Inputs may be any that keep to these rules, and one draw needn't show every extreme that they name: `doc_ids`: Non-decreasing along the sequence; every document has 1024 tokens at most, and some document exactly 1024.
All inputs are finite; a program needn't handle non-finite values.
Results may differ from a plain program's by a relative error of at most 0.0034.
Values may be sent and summed in bfloat16 or wider, within the bound.
A program may use at most 64 MiB of HBM per device.

v0:
```python
import functools
import math

import jax
import jax.numpy as jnp
from jax import lax
from jax.experimental import pallas as pl
from jax.experimental.pallas import tpu as pltpu
from jax.sharding import PartitionSpec as P

HEAD_WIDTH = 128
DOC_BLKS = 4
MESH = pl.DeviceIdType.MESH
NEG = -1e30


def kernel(n, q_hbm, k_hbm, v_hbm, doc_hbm, o_ref,
           qbuf, kv, docs, bias, mref, lref, acc,
           qsem, loadsem, docsem, docsend, docrecv, send, recv):
    rows = q_hbm.shape[0]
    kv_heads = k_hbm.shape[1] // HEAD_WIDTH
    heads = q_hbm.shape[1] // HEAD_WIDTH
    group = heads // kv_heads
    chunks = 2 * kv_heads
    scale = math.log2(math.e) / math.sqrt(HEAD_WIDTH)

    me = lax.axis_index("blk")
    core = lax.rem(me, 2)
    pair = me // 2
    pairs = n // 2

    def load(i):
        src = (k_hbm, v_hbm)[i % 2].at[:, pl.ds((i // 2) * HEAD_WIDTH, HEAD_WIDTH)]
        return pltpu.make_async_copy(src, kv.at[0, i], loadsem.at[i])

    def load_q(h):
        return pltpu.make_async_copy(q_hbm.at[:, pl.ds(h * HEAD_WIDTH, HEAD_WIDTH)], qbuf.at[h], qsem.at[h])

    load_doc = pltpu.make_async_copy(doc_hbm, docs.at[0], docsem)
    for i in range(chunks):
        load(i).start()
    load_doc.start()
    for h in range(heads):
        load_q(h).start()

    barrier = pltpu.get_barrier_semaphore()
    for o in range(1, DOC_BLKS + 1):
        @pl.when(me + o < n)
        def _():
            pl.semaphore_signal(barrier, inc=1, device_id={"blk": me + o}, device_id_type=MESH)

        @pl.when(me >= o)
        def _():
            pl.semaphore_signal(barrier, inc=1, device_id={"blk": me - o}, device_id_type=MESH)
    pl.semaphore_wait(barrier, jnp.minimum(me, DOC_BLKS) + jnp.minimum(n - 1 - me, DOC_BLKS))

    def doc_copy(o):
        return pltpu.make_async_remote_copy(
            src_ref=docs.at[0], dst_ref=docs.at[o], send_sem=docsend.at[o], recv_sem=docrecv.at[o],
            device_id={"blk": me + o}, device_id_type=MESH)

    def copy(src_slot, dst_slot, i, step):
        return pltpu.make_async_remote_copy(
            src_ref=kv.at[src_slot, i], dst_ref=kv.at[dst_slot, i],
            send_sem=send.at[src_slot, dst_slot, i], recv_sem=recv.at[dst_slot, i],
            device_id={"blk": me + step}, device_id_type=MESH)

    far = me + 4 < n
    relayed_source = (lax.rem(pair, 4) == 1) & (pair + 2 < pairs)
    skips = (me + 2 < n) & relayed_source
    near = (me + 2 < n) & jnp.logical_not(relayed_source)
    relays = lax.rem(pair, 4) == 3
    late = (lax.rem(pair, 4) == 2) & (pair + 1 < pairs)
    has4 = me >= 4
    has2 = me >= 2
    own_flows = [(far, 0, 4, 4), (near, 0, 2, 2), (core == 0, 0, 1, 1)]
    four_flows = [(has4 & relays, 4, 2, -2), (has4 & (core == 1), 4, 3, -1)]
    two_flows = [(has2 & (core == 0), 2, 3, 1), (has2 & (core == 1), 2, 1, -1)]

    def start(flows, i):
        for cond, s, d, step in flows:
            if step == -2 and i == chunks - 1:
                continue
            @pl.when(cond)
            def _():
                copy(s, d, i, step).start()

    def arrived(slot, i):
        pltpu.make_async_remote_copy(
            src_ref=kv.at[0, i], dst_ref=kv.at[slot, i], send_sem=send.at[0, 1, i], recv_sem=recv.at[slot, i],
            device_id={"blk": lax.rem(me + 1, n)}, device_id_type=MESH).wait_recv()

    for i in range(chunks):
        load(i).wait()
        start(own_flows, i)
        if i == 0:
            load_doc.wait()
            for o in range(1, DOC_BLKS + 1):
                @pl.when(me + o < n)
                def _():
                    doc_copy(o).start()

    def column(row):
        return jnp.broadcast_to(row, (HEAD_WIDTH, rows)).T

    def make_bias(o):
        key_docs = column(docs[o, 0:1, :])
        for c in range(rows // HEAD_WIDTH):
            cols = slice(c * HEAD_WIDTH, (c + 1) * HEAD_WIDTH)
            ok = key_docs == docs[0, 0:1, cols]
            if o == 0:
                s = lax.broadcasted_iota(jnp.int32, (rows, HEAD_WIDTH), 0)
                r = lax.broadcasted_iota(jnp.int32, (rows, HEAD_WIDTH), 1) + c * HEAD_WIDTH
                ok = ok & (s <= r)
            bias[o, :, cols] = jnp.where(ok, 0.0, NEG)

    def own(o):
        return isinstance(o, int) and o == 0

    def scores(o, h):
        g = h // group
        if own(o):
            load_q(h).wait()
        s = lax.dot_general(kv[o, 2 * g], qbuf[h], (((1,), (1,)), ((), ())),
                            preferred_element_type=jnp.float32)
        s = s + bias[o]
        return s, jnp.max(s, axis=0, keepdims=True)

    def weigh(o, h, s, m, values_t):
        if not own(o):
            old = mref[h]
            m = jnp.maximum(m, old)
            alpha = jnp.exp2((old - m) * scale)
        w = jnp.exp2(s * scale - m * scale)
        l = jnp.sum(w, axis=0, keepdims=True)
        a = jnp.dot(values_t, w.astype(jnp.bfloat16), preferred_element_type=jnp.float32)
        if not own(o):
            l = l + lref[h] * alpha
            a = a + acc[h] * alpha
        mref[h] = m
        lref[h] = l
        acc[h] = a

    def attend(o, groups):
        todo = [h for g in groups for h in range(g * group, (g + 1) * group)]
        values_t = {g: kv[o, 2 * g + 1].T for g in groups}
        held = scores(o, todo[0])
        for k, h in enumerate(todo):
            ahead = scores(o, todo[k + 1]) if k + 1 < len(todo) else None
            weigh(o, h, *held, values_t[h // group])
            held = ahead

    make_bias(0)
    attend(0, range(kv_heads))

    def receive_docs(o):
        @pl.when(me >= o)
        def _():
            doc_copy(o).wait_recv()
            make_bias(o)

    receive_docs(1)
    @pl.when(core == 1)
    def _():
        for i in range(chunks):
            arrived(1, i)
        attend(1, range(kv_heads))

    def take(cond, slot, flows, i):
        @pl.when(cond)
        def _():
            arrived(slot, i)
        start(flows(i), i) if callable(flows) else start(flows, i)

    prompt2 = has2 & jnp.logical_not(late)
    late2 = has2 & late

    def with_cond(cond, flows):
        return [(cond & c, s, d, step) for c, s, d, step in flows]

    for o in range(2, DOC_BLKS + 1):
        receive_docs(o)

    for g in range(kv_heads):
        for i in (2 * g, 2 * g + 1):
            take(has4, 4, four_flows, i)
            take(prompt2, 2, with_cond(prompt2, two_flows), i)

        if g == 0:
            @pl.when(skips)
            def _():
                copy(0, 2, chunks - 1, 2).start()

        @pl.when(has4)
        def _():
            attend(4, [g])

        @pl.when(has4 & (core == 0))
        def _():
            for i in (2 * g, 2 * g + 1):
                arrived(3, i)
            attend(3, [g])

    last = jnp.where(core == 0, 1, 3)
    for g in range(kv_heads):
        for i in (2 * g, 2 * g + 1):
            take(late2, 2, with_cond(late2, two_flows), i)

        @pl.when(has2)
        def _():
            attend(2, [g])
            for i in (2 * g, 2 * g + 1):
                arrived(last, i)
            attend(last, [g])

    @pl.when(skips)
    def _():
        copy(0, 2, chunks - 1, 2).wait_send()

    for h in range(heads):
        o_ref[:, h * HEAD_WIDTH:(h + 1) * HEAD_WIDTH] = (acc[h] / lref[h]).T.astype(o_ref.dtype)

    for o in range(1, DOC_BLKS + 1):
        @pl.when(me + o < n)
        def _():
            doc_copy(o).wait_send()
    for cond, s, d, step in own_flows + four_flows + two_flows:
        @pl.when(cond)
        def _():
            for i in range(chunks - (step == -2)):
                copy(s, d, i, step).wait_send()


def shards(n, queries, keys, values, doc_ids):
    rows = queries.shape[0]
    heads = queries.shape[1] // HEAD_WIDTH
    chunks = 2 * (keys.shape[1] // HEAD_WIDTH)
    slots = DOC_BLKS + 1
    hbm_spec = pl.BlockSpec(memory_space=pltpu.HBM)
    stat = pltpu.VMEM((heads, 1, rows), jnp.float32)
    return pl.pallas_call(
        functools.partial(kernel, n),
        out_shape=pltpu.VMEM(queries.shape, jnp.bfloat16),
        in_specs=[hbm_spec] * 4,
        out_specs=pl.BlockSpec(memory_space=pltpu.VMEM),
        scratch_shapes=[
            pltpu.VMEM((heads, rows, HEAD_WIDTH), jnp.bfloat16),
            pltpu.VMEM((slots, chunks, rows, HEAD_WIDTH), jnp.bfloat16),
            pltpu.VMEM((slots, 1, rows), jnp.int32),
            pltpu.VMEM((slots, rows, rows), jnp.float32),
            stat, stat,
            pltpu.VMEM((heads, HEAD_WIDTH, rows), jnp.float32),
            pltpu.SemaphoreType.DMA((heads,)),
            pltpu.SemaphoreType.DMA((chunks,)),
            pltpu.SemaphoreType.DMA,
            pltpu.SemaphoreType.DMA((slots,)),
            pltpu.SemaphoreType.DMA((slots,)),
            pltpu.SemaphoreType.DMA((slots, slots, chunks)),
            pltpu.SemaphoreType.DMA((slots, chunks)),
        ],
        compiler_params=pltpu.CompilerParams(collective_id=0, has_side_effects=True,
                                             vmem_limit_bytes=24 * 2**20),
    )(*(pltpu.with_memory_space_constraint(x, pltpu.HBM) for x in (queries, keys, values, doc_ids.reshape(1, rows))))


def solution(mesh):
    return jax.shard_map(
        functools.partial(shards, mesh.shape["blk"]),
        mesh=mesh,
        in_specs=(P("blk", "heads"), P("blk", "heads"), P("blk", "heads"), P("blk")),
        out_specs=P("blk", "heads"),
        check_vma=False,
    )
```

profile of v0, /device:TPU:13, one launch (start us, length us, event | category | flops | bytes accessed | tf_op | source)
XLA Modules:
  0.0 17.6 jit_solution(11025703021493457592)
XLA Ops:
  0.0 16.8 %shard_map.46 = bf16[256,1024]{1,0:T(8,128)(2,1)S(1)} custom-call(bf16[256,1024]{1,0:T(8,128)(2,1)} %q_hbm.1, bf16[256,256]{1,0:T(8,128)(2,1)} %k_hbm.1, bf16[256,256]{1,0:T(8,128)(2,1)} %v_hbm.1, s32[1,256]{1,0:T(1,128)} %bitcast.1), custom_call_target="tpu_custom_call" | custom-call | tf_op jit(solution)/shard_map/pallas_call | solution.py:241
  16.8 0.8 %copy.6 = bf16[256,1024]{1,0:T(8,128)(2,1)} copy(bf16[256,1024]{1,0:T(8,128)(2,1)S(1)} %shard_map.46) | data formatting | bytes 1048576
where the time goes:
time: 17.8 us; the launch traced here: 17.6 us
  Pallas kernels  16.8 us (94%)
  local copies, waits for them, and re-layouts  0.8 us (4%)
    pallas_call x1, Pallas kernels, shards(): pl.pallas_call(functools.partial(kernel, n), out_shape=pltpu.VMEM(queries...  16.8 us
    unnamed x1, local copies, waits for them, and re-layouts  0.8 us

commit v1 on v0

v1 whole, which is shorter than its diff:
```python
import functools
import math

import jax
import jax.numpy as jnp
from jax import lax
from jax.experimental import pallas as pl
from jax.experimental.pallas import tpu as pltpu
from jax.sharding import PartitionSpec as P

HEAD_WIDTH = 128
DOC_BLKS = 4
MESH = pl.DeviceIdType.MESH
NEG = -1e30
S_SLOTS = 2
P_SLOTS = 4
scope = jax.named_scope


def fold(x, op, chains=4):
    parts = jnp.split(x, chains, axis=0)
    while len(parts) > 1:
        parts = [op(a, b) for a, b in zip(parts[::2], parts[1::2])]
    return parts[0]


def kernel(n, q_hbm, k_hbm, v_hbm, doc_hbm, o_ref,
           qbuf, qt, kv, docs, bias, mref, lref, acc, sbuf, mbuf, pbuf, abuf,
           qsem, loadsem, docsem, docsend, docrecv, send, recv):
    rows = q_hbm.shape[0]
    kv_heads = k_hbm.shape[1] // HEAD_WIDTH
    heads = q_hbm.shape[1] // HEAD_WIDTH
    group = heads // kv_heads
    chunks = 2 * kv_heads
    scale = math.log2(math.e) / math.sqrt(HEAD_WIDTH)

    me = lax.axis_index("blk")
    core = lax.rem(me, 2)
    pair = me // 2
    pairs = n // 2

    def columns(h):
        return slice(h * HEAD_WIDTH, (h + 1) * HEAD_WIDTH)

    load_q = pltpu.make_async_copy(q_hbm, qbuf, qsem)
    load_doc = pltpu.make_async_copy(doc_hbm, docs.at[0], docsem)
    for i in range(chunks):
        src = (k_hbm, v_hbm)[i % 2].at[:, pl.ds((i // 2) * HEAD_WIDTH, HEAD_WIDTH)]
        pltpu.make_async_copy(src, kv.at[0, i], loadsem).start()
    load_doc.start()
    load_q.start()

    far = me + 4 < n
    relayed_source = (lax.rem(pair, 4) == 1) & (pair + 2 < pairs)
    skips = (me + 2 < n) & relayed_source
    near = (me + 2 < n) & jnp.logical_not(relayed_source)
    late = (lax.rem(pair, 4) == 2) & (pair + 1 < pairs)
    has4 = me >= 4
    has2 = me >= 2
    relays = has4 & (lax.rem(pair, 4) == 3)

    barrier = pltpu.get_barrier_semaphore()

    def greet(cond, step):
        @pl.when(cond)
        def _():
            pl.semaphore_signal(barrier, inc=1, device_id={"blk": me + step}, device_id_type=MESH)

    for o in range(1, DOC_BLKS + 1):
        greet(me >= o, -o)
    greet(core == 0, 1)
    greet(late, 2)
    with scope("barrier"):
        pl.semaphore_wait(barrier, jnp.minimum(n - 1 - me, DOC_BLKS) + core + relays.astype(jnp.int32))

    def doc_copy(o):
        return pltpu.make_async_remote_copy(
            src_ref=docs.at[0], dst_ref=docs.at[o], send_sem=docsend.at[o - 1], recv_sem=docrecv.at[o - 1],
            device_id={"blk": me + o}, device_id_type=MESH)

    FAR, NEAR, OWN, BACK, FOUR, TWO = range(6)
    half = rows // 2
    K0, V0, K1, V1 = range(4)

    def piece(slot, i, part):
        if part is None:
            return kv.at[slot, i]
        return kv.at[slot, i, pl.ds(part * half, half)]

    def arrival(slot, i, part):
        base = {4: 0, 2: 2 * chunks, 3: 4 * chunks, 1: 5 * chunks}
        if slot in (4, 2):
            return recv.at[base[slot] + 2 * i + (part or 0)]
        return recv.at[base[slot] + i]

    def copy(flow, i, part=None):
        if flow == TWO:
            src, dst, step = 2, jnp.where(core == 0, 3, 1), 1 - 2 * core
            sem = recv.at[jnp.where(core == 0, 4 * chunks, 5 * chunks) + i]
        else:
            src, dst, step = {FAR: (0, 4, 4), NEAR: (0, 2, 2), OWN: (0, 1, 1), BACK: (4, 2, -2), FOUR: (4, 3, -1)}[flow]
            sem = arrival(dst, i, part)
        return pltpu.make_async_remote_copy(
            src_ref=piece(src, i, part), dst_ref=piece(dst, i, part),
            send_sem=send.at[flow], recv_sem=sem,
            device_id={"blk": me + step}, device_id_type=MESH)

    def push(cond, flow, i, part=None):
        @pl.when(cond)
        def _():
            copy(flow, i, part).start()

    def arrived(slot, i, part=None):
        pltpu.make_async_remote_copy(
            src_ref=piece(0, i, part), dst_ref=piece(slot, i, part), send_sem=send.at[OWN],
            recv_sem=arrival(slot, i, part),
            device_id={"blk": lax.rem(me + 1, n)}, device_id_type=MESH).wait_recv()

    load_doc.wait()
    for o in range(1, DOC_BLKS + 1):
        @pl.when(me + o < n)
        def _():
            doc_copy(o).start()

    with scope("ld"):
        pltpu.make_async_copy(kv.at[1], kv.at[0], loadsem).wait()
    third = jnp.where(relayed_source, V1, K1)
    fourth = jnp.where(relayed_source, K1, V1)
    for i in (K0, V0, third, fourth):
        for part in range(2):
            push(far, FAR, i, part)
        push(near, NEAR, i)
        if i is K0 or i is V0:
            push(core == 0, OWN, i)
    push(core == 0, OWN, K1)
    push(core == 0, OWN, V1)
    push(skips, NEAR, K1)

    def column(row):
        return jnp.broadcast_to(row, (HEAD_WIDTH, rows)).T

    def make_bias(o):
        key_docs = column(docs[o, 0:1, :])
        for c in range(rows // HEAD_WIDTH):
            cols = columns(c)
            ok = key_docs == docs[0, 0:1, cols]
            if isinstance(o, int) and o == 0:
                s = lax.broadcasted_iota(jnp.int32, (rows, HEAD_WIDTH), 0)
                r = lax.broadcasted_iota(jnp.int32, (rows, HEAD_WIDTH), 1) + c * HEAD_WIDTH
                ok = ok & (s <= r)
            bias[o, :, cols] = jnp.where(ok, 0.0, NEG)

    def scores(o, h):
        k = kv[o, 2 * (h // group)]
        s = jnp.dot(jnp.concatenate([k, k], axis=1), qt[h], preferred_element_type=jnp.float32) + bias[o]
        return s, jnp.max(fold(s, jnp.maximum), axis=0, keepdims=True)

    def weigh(o, h, s, m):
        alpha = None
        if o != 0:
            old = mref[h]
            m = jnp.maximum(m, old)
            alpha = jnp.exp2(old - m)
        w = jnp.exp2(s - m)
        l = jnp.sum(fold(w, jnp.add), axis=0, keepdims=True)
        if o != 0:
            l = l + lref[h] * alpha
        mref[h] = m
        lref[h] = l
        return w.astype(jnp.bfloat16), alpha

    def gather(o, h, w, alpha, values_t):
        a = jnp.dot(values_t, w, preferred_element_type=jnp.float32)
        acc[h] = a if o == 0 else a + acc[h] * alpha

    def attend(o, batch=2):
        values_t = {}
        scored, weighed = {}, {}
        for t in range(0, heads + 2 * batch, batch):
            for h in range(t, t + batch):
                if h < heads:
                    scored[h] = scores(o, h)
                h -= 2 * batch
                if h >= 0:
                    g = h // group
                    if g not in values_t:
                        values_t[g] = kv[o, 2 * g + 1].T
                    gather(o, h, *weighed.pop(h), values_t[g])
                h += batch
                if 0 <= h < heads:
                    weighed[h] = weigh(o, h, *scored.pop(h))

    def do(A=(), B=(), C=(), fin=()):
        name = "".join("A%d%d" % t for t in A) + "".join("B%d%d" % t for t in B) + "".join("C%d%d" % t for t in C)
        with scope(name):
            values_t = {t: kv[t[0], 2 * t[1] + 1].T for t in C}
            for j in range(group):
                for t in A:
                    s, m = scores(t[0], t[1] * group + j)
                    sbuf[s_slot[t], j] = s
                    mbuf[s_slot[t], j] = m
                for t in C:
                    w = p_slot[t]
                    gather(t[0], t[1] * group + j, pbuf[w, j], abuf[w, j], values_t[t])
                for t in B:
                    x = s_slot[t]
                    w, alpha = weigh(t[0], t[1] * group + j, sbuf[x, j], mbuf[x, j])
                    pbuf[p_slot[t], j] = w
                    abuf[p_slot[t], j] = alpha
            for g in fin:
                finish(g)

    def finish(g):
        for h in range(g * group, (g + 1) * group):
            o_ref[:, columns(h)] = (acc[h] / lref[h]).T.astype(o_ref.dtype)

    s_slot, p_slot = {}, {}

    def plan(steps):
        s_slot.clear()
        p_slot.clear()
        free_s, free_p = list(range(S_SLOTS)), list(range(P_SLOTS))
        for step in steps:
            for t in step.get("B", ()):
                p_slot[t] = free_p.pop(0)
            for t in step.get("A", ()):
                s_slot[t] = free_s.pop(0)
            free_s += [s_slot[t] for t in step.get("B", ())]
            free_p += [p_slot[t] for t in step.get("C", ())]

    def receive(event):
        kind, i = event[0], event[1]
        part = event[2] if len(event) > 2 else None
        with scope("w" + "".join(str(e) for e in event)):
            arrived(kind, i, part)
        if kind == 4:
            if i != K1 and part is not None:
                push(relays, BACK, i, part)

    def run(steps):
        plan(steps)
        for step in steps:
            for event in step.get("W", ()):
                if event[0] == "f4":
                    push(core == 1, FOUR, event[1])
                elif event[0] == "f2":
                    copy(TWO, event[1]).start()
                else:
                    receive(event)
            rest = {k: v for k, v in step.items() if k != "W"}
            if rest:
                do(**rest)

    with scope("ldq"):
        load_q.wait()
    with scope("prep"):
        for h in range(heads):
            x = qbuf[:, columns(h)].T.astype(jnp.float32) * scale
            hi = x.astype(jnp.bfloat16)
            qt[h, :HEAD_WIDTH] = hi
            qt[h, HEAD_WIDTH:] = (x - hi.astype(jnp.float32)).astype(jnp.bfloat16)
        make_bias(0)
    with scope("own"):
        attend(0)

    def receive_docs(o):
        @pl.when(me >= o)
        def _():
            doc_copy(o).wait_recv()
            make_bias(o)

    with scope("docs1"):
        receive_docs(1)

    @pl.when(core == 1)
    def _():
        with scope("w1"):
            for i in range(chunks):
                arrived(1, i)
        with scope("a1"):
            attend(1)

    with scope("docs"):
        for o in range(2, DOC_BLKS + 1):
            receive_docs(o)

    def role(cond, steps):
        @pl.when(cond)
        def _():
            run(steps)

    def w4(i):
        return [(4, i, 0), (4, i, 1), ("f4", i)]

    def w2(i):
        return [(2, i), ("f2", i)]

    def w2r(i):
        return [(2, i, 0), (2, i, 1), ("f2", i)]

    t = lambda *names: [(int(x[0]), int(x[1])) for x in names]
    S = lambda W=(), A=(), B=(), C=(), fin=(): {k: v for k, v in dict(W=list(W), A=t(*A), B=t(*B), C=t(*C), fin=fin).items() if v}

    role(has4 & late & (core == 0), [
        S(w4(K0), ["40"]),
        S([(3, K0)], ["30"], ["40"]),
        S(w4(V0), [], ["30"], ["40"]),
        S([(3, V0)], [], [], ["30"]),
        S(w2r(K0), ["20"]),
        S(w4(K1), ["41"], ["20"]),
        S(w2(K1) + [(1, K0)], ["10"], ["41"]),
        S([], ["21"], ["10"]),
        S(w2r(V0) + [(3, K1)], ["31"], ["21"], ["20"]),
        S([(1, K1), (1, V0)], ["11"], ["31"], ["10"]),
        S(w4(V1) + w2r(V1), [], ["11"], ["41", "21"], [0]),
        S([(3, V1), (1, V1)], [], [], ["31", "11"], [1]),
    ])
    role(has4 & late & (core == 1), [
        S(w4(K0), ["40"]),
        S(w4(V0), [], ["40"], ["40"]) if False else S([], [], ["40"]),
        S(w4(V0), [], [], ["40"]),
        S(w2r(K0), ["20"]),
        S(w4(K1), ["41"], ["20"]),
        S(w2(K1) + [(3, K0)], ["30"], ["41"]),
        S([], ["21"], ["30"]),
        S(w2r(V0), [], ["21"], ["20"]),
        S([(3, K1), (3, V0)], ["31"], [], ["30"]),
        S(w4(V1) + w2r(V1), [], ["31"], ["41", "21"], [0]),
        S([(3, V1)], [], [], ["31"], [1]),
    ])
    role(has4 & jnp.logical_not(late) & (core == 0), [
        S(w4(K0) + w2(K0), ["40"]),
        S([], ["20"], ["40"]),
        S([(4, V0, 0), (3, K0)], ["30"], ["20"]),
        S([(4, V0, 1), ("f4", V0)] + w2(V0) + [(1, K0)], ["10"], ["30"], ["40"]),
        S([(4, V1, 0)], [], ["10"], ["20"]),
        S([(4, V1, 1), ("f4", V1), (3, V0), (1, V0)], [], [], ["30", "10"], [0]),
        S(w2(K1), ["21"]),
        S(w4(K1), ["41"], ["21"]),
        S(w2(V1) + [(1, K1)], ["11"], ["41"], ["21"]),
        S([(3, K1)], ["31"], ["11"], ["41"]),
        S([(1, V1)], [], ["31"], ["11"]),
        S([(3, V1)], [], [], ["31"], [1]),
    ])
    role(has4 & jnp.logical_not(late) & (core == 1), [
        S(w4(K0) + w2(K0), ["40"]),
        S([], ["20"], ["40"]),
        S([(4, V0, 0), (3, K0)], ["30"], ["20"]),
        S([(4, V0, 1), ("f4", V0)] + w2(V0), [], ["30"], ["40", "20"]),
        S([(4, V1, 0)]),
        S([(4, V1, 1), ("f4", V1), (3, V0)], [], [], ["30"], [0]),
        S(w2(K1), ["21"]),
        S(w4(K1), ["41"], ["21"]),
        S(w2(V1) + [(3, K1)], ["31"], ["41"], ["21"]),
        S([], [], ["31"], ["41"]),
        S([(3, V1)], [], [], ["31"], [1]),
    ])
    for c, a in ((0, "1"), (1, "3")):
        b = int(a)
        role(has2 & jnp.logical_not(has4) & (core == c), [
            S(w2(K0), ["20"]),
            S([(b, K0)], [a + "0"], ["20"]),
            S(w2(V0), [], [a + "0"], ["20"]),
            S([(b, V0)], [], [], [a + "0"], [0]),
            S(w2(K1), ["21"]),
            S([(b, K1)], [a + "1"], ["21"]),
            S(w2(V1), [], [a + "1"], ["21"]),
            S([(b, V1)], [], [], [a + "1"], [1]),
        ])

    @pl.when(me < 2)
    def _():
        for g in range(kv_heads):
            finish(g)

    with scope("end"):
        for o in range(1, DOC_BLKS + 1):
            @pl.when(me + o < n)
            def _():
                doc_copy(o).wait_send()

        def sent(cond, flow, i):
            @pl.when(cond)
            def _():
                pltpu.make_async_remote_copy(
                    src_ref=kv.at[0, i], dst_ref=kv.at[1, i], send_sem=send.at[flow], recv_sem=recv.at[0],
                    device_id={"blk": lax.rem(me + 1, n)}, device_id_type=MESH).wait_send()

        full = slice(None)
        sent(skips, NEAR, K1)
        sent(near, NEAR, full)
        sent(far, FAR, full)
        sent(core == 0, OWN, full)
        sent(relays, BACK, pl.ds(0, chunks - 1))
        sent(has4 & (core == 1), FOUR, full)
        sent(has2, TWO, full)


def shards(n, queries, keys, values, doc_ids):
    rows = queries.shape[0]
    heads = queries.shape[1] // HEAD_WIDTH
    chunks = 2 * (keys.shape[1] // HEAD_WIDTH)
    group = heads * HEAD_WIDTH // keys.shape[1]
    slots = DOC_BLKS + 1
    hbm_spec = pl.BlockSpec(memory_space=pltpu.HBM)
    stat = pltpu.VMEM((heads, 1, rows), jnp.float32)
    return pl.pallas_call(
        functools.partial(kernel, n),
        out_shape=pltpu.VMEM(queries.shape, jnp.bfloat16),
        in_specs=[hbm_spec] * 4,
        out_specs=pl.BlockSpec(memory_space=pltpu.VMEM),
        scratch_shapes=[
            pltpu.VMEM(queries.shape, jnp.bfloat16),
            pltpu.VMEM((heads, 2 * HEAD_WIDTH, rows), jnp.bfloat16),
            pltpu.VMEM((slots, chunks, rows, HEAD_WIDTH), jnp.bfloat16),
            pltpu.VMEM((slots, 1, rows), jnp.int32),
            pltpu.VMEM((slots, rows, rows), jnp.float32),
            stat, stat,
            pltpu.VMEM((heads, HEAD_WIDTH, rows), jnp.float32),
            pltpu.VMEM((S_SLOTS, group, rows, rows), jnp.float32),
            pltpu.VMEM((S_SLOTS, group, 1, rows), jnp.float32),
            pltpu.VMEM((P_SLOTS, group, rows, rows), jnp.bfloat16),
            pltpu.VMEM((P_SLOTS, group, 1, rows), jnp.float32),
            pltpu.SemaphoreType.DMA,
            pltpu.SemaphoreType.DMA,
            pltpu.SemaphoreType.DMA,
            pltpu.SemaphoreType.DMA((DOC_BLKS,)),
            pltpu.SemaphoreType.DMA((DOC_BLKS,)),
            pltpu.SemaphoreType.DMA((6,)),
            pltpu.SemaphoreType.DMA((6 * chunks,)),
        ],
        compiler_params=pltpu.CompilerParams(collective_id=0, has_side_effects=True,
                                             vmem_limit_bytes=32 * 2**20),
    )(*(pltpu.with_memory_space_constraint(x, pltpu.HBM) for x in (queries, keys, values, doc_ids.reshape(1, rows))))


def solution(mesh):
    return jax.shard_map(
        functools.partial(shards, mesh.shape["blk"]),
        mesh=mesh,
        in_specs=(P("blk", "heads"), P("blk", "heads"), P("blk", "heads"), P("blk")),
        out_specs=P("blk", "heads"),
        check_vma=False,
    )
```

time: 17.8 us -> 14.8 us (0.83)
  Pallas kernels: 16.8 us -> 13.9 us
    pallas_call x1, Pallas kernels: 16.8 us -> 13.9 us  [shards(): pl.pallas_call(functools.partial(kernel, n), out_shape=pltpu.VMEM(queries...]
where the time goes in v1:
time: 14.8 us; the launch traced here: 14.7 us
  Pallas kernels  13.9 us (94%)
  local copies, waits for them, and re-layouts  0.8 us (5%)
    pallas_call x1, Pallas kernels, shards(): pl.pallas_call(functools.partial(kernel, n), out_shape=pltpu.VMEM(queries...  13.9 us
    unnamed x1, local copies, waits for them, and re-layouts  0.8 us

profile of v1, /device:TPU:13, one launch (start us, length us, event | category | flops | bytes accessed | tf_op | source)
XLA Modules:
  0.0 14.7 jit_solution(7334982361382954215)
XLA Ops:
  0.0 13.9 %shard_map.46 = bf16[256,1024]{1,0:T(8,128)(2,1)S(1)} custom-call(bf16[256,1024]{1,0:T(8,128)(2,1)} %q_hbm.1, bf16[256,256]{1,0:T(8,128)(2,1)} %k_hbm.1, bf16[256,256]{1,0:T(8,128)(2,1)} %v_hbm.1, s32[1,256]{1,0:T(1,128)} %bitcast.1), custom_call_target="tpu_custom_call" | custom-call | tf_op jit(solution)/shard_map/pallas_call | solution.py:407
  13.9 0.8 %copy.6 = bf16[256,1024]{1,0:T(8,128)(2,1)} copy(bf16[256,1024]{1,0:T(8,128)(2,1)S(1)} %shard_map.46) | data formatting | bytes 1048576
